TPU v7x, 32 devices: a whole 2x2x4 slice. The times are simulated.
32 devices in a mesh: gz: 4 (over y, x), gy: 4 (over z), gx: 2 (over core).
Axes of the slice: x: 2, y: 2, z: 4, core: 2. Of those that a mesh axis runs over, the one named last changes fastest.
Arguments:
- spins: float32 [2, 64, 192, 256], P(None, 'gz', 'gy', 'gx'), may hold values from -6 to 6
- kicks: float32 [2, 2, 64, 192, 256], P(None, None, 'gz', 'gy', 'gx'), may hold values from -6 to 6
- stiffness: float32 [64, 192, 256], P('gz', 'gy', 'gx'), may hold values from 0.1 to 11, as said below
Outputs:
- final_spins: float32 [2, 64, 192, 256], P(None, 'gz', 'gy', 'gx')
- section_energy: float32 [16], replicated
Inputs may be any that keep to these rules, and one draw needn't show every extreme that they name: `stiffness`: positive coupling strengths.
All inputs are finite; a program needn't handle non-finite values.
Results may differ from a plain program's by a relative error of at most 0.0001.
Values sent between devices are 32-bit elements; how exact they have to be, the bound alone decides.
No kernel may reach another device: no remote copies, remote signals or barrier semaphores. Data moves between devices by JAX's collectives and lax.ppermute only.
A program may use at most 128 MiB of HBM per device.

v0:
```python
import functools

import jax
import jax.numpy as jnp
from jax import lax
from jax.experimental import pallas as pl
from jax.experimental.pallas import tpu as pltpu
from jax.sharding import PartitionSpec as P


SWEEPS = 2
FACE_GRANT = 55_000_000
EDGE_GRANT = 8_000_000
VMEM = pl.BlockSpec(memory_space=pltpu.VMEM)
F32 = jnp.float32

FIRST = (0, 1, 2, 3, 4)
ALL = (0, 1, 2, 3, 4, 5, 6)


def up_planes(depth):
    return [(f, z) for f in FIRST for z in (depth - 2, depth - 1)]


def down_planes():
    return [(f, z) for f in FIRST for z in (0, 1, 2)] + [(5, 0), (6, 0)]


CORNERS = {"cuu": 0, "cud": 5, "cdu": 10, "cdd": 19, "end": 28}


def load_field(s_ref, k_ref, st_ref, field, z, rows=slice(None)):
    return field_ref(s_ref, k_ref, st_ref, field)[z, rows, :]


def field_ref(s_ref, k_ref, st_ref, field):
    if field < 2:
        return s_ref.at[field]
    if field == 2:
        return st_ref
    return k_ref.at[(field - 3) // 2, (field - 3) % 2]


def copy_all(moves, sems):
    copies = [pltpu.make_async_copy(a, b, sems.at[i]) for i, (a, b) in enumerate(moves)]
    for c in copies:
        c.start()
    for c in copies:
        c.wait()


def face_kernel(s_ref, k_ref, st_ref, zup, zdn, far, sems):
    depth, _, _ = st_ref.shape
    get = functools.partial(field_ref, s_ref, k_ref, st_ref)
    moves = [(s_ref.at[:, depth - 3], far.at[0]), (s_ref.at[:, 3], far.at[1])]
    for f in FIRST:
        moves.append((get(f).at[pl.ds(0, 3)], zdn.at[pl.ds(3 * f, 3)]))
        moves.append((get(f).at[pl.ds(depth - 2, 2)], zup.at[pl.ds(2 * f, 2)]))
    moves += [(get(5).at[pl.ds(0, 1)], zdn.at[pl.ds(15, 1)]), (get(6).at[pl.ds(0, 1)], zdn.at[pl.ds(16, 1)])]
    copy_all(moves, sems)
    for c in (0, 1):
        n = 2 * (3 + c)
        zup[n] = zup[n] + zup[4] * far[0, c]
        n = 3 * (3 + c) + 2
        zdn[n] = zdn[n] + zdn[8] * far[1, c]


def edge_kernel(s_ref, k_ref, st_ref, zup, zdn, up, down, corners, s_low, s_high, k_low, k_high, t_low, t_high, sems):
    depth, height, lanes = st_ref.shape
    first, last = pl.ds(0, 8), pl.ds(height - 8, 8)
    copy_all(
        [
            (s_ref.at[:, :, first], s_low),
            (s_ref.at[:, :, last], s_high),
            (k_ref.at[:, :, :, first], k_low),
            (k_ref.at[0, :, :, last], k_high),
            (st_ref.at[:, first], t_low),
            (st_ref.at[:, last], t_high),
        ],
        sems,
    )
    sub = lax.broadcasted_iota(jnp.int32, (8, lanes), 0)
    quad = sub % 4
    order = (quad % 2) * 2 + quad // 2
    lower = sub < 4

    def merge(a, b, base):
        a = jnp.take_along_axis(a, order + base, axis=0)
        b = jnp.take_along_axis(b, order + base, axis=0)
        return jnp.where(lower, a, b)

    at = CORNERS
    for src, hi, lo, count in ((zup, at["cud"], at["cuu"], 10), (zdn, at["cdd"], at["cdu"], 17)):
        for n in range(0, count, 2):
            m = min(n + 1, count - 1)
            corners[hi + n // 2] = merge(src[n, first, :], src[m, first, :], 0)
            corners[lo + n // 2] = merge(src[n, last, :], src[m, last, :], 4)

    def row(field, z, is_low):
        s, k, t = (s_low, k_low, t_low) if is_low else (s_high, k_high, t_high)
        if field < 2:
            return s[field, z]
        if field == 2:
            return t[z]
        c = (field - 3) % 2
        if not is_low:
            return k[c, z] + jnp.where(sub == 6, t[z] * pltpu.roll(s[c, z], 1, 0), 0.0)
        if field > 4:
            return k[1, c, z]
        return k[0, c, z] + jnp.where(sub == 2, t[z] * pltpu.roll(s[c, z], 7, 0), 0.0)

    for field in FIRST:
        for p in range(depth // 2):
            tile = merge(row(field, 2 * p, True), row(field, 2 * p + 1, True), 0)
            if field < 2:
                a, b = (pltpu.roll(row(5 + field, 2 * p + i, True), 3 + 4 * i, 0) for i in (0, 1))
                tile = jnp.where(quad == 3, jnp.where(lower, a, b), tile)
            down[field * (depth // 2) + p] = tile
        for q in range(depth // 4):
            tile = row(field, 4 * q + 3, False)
            for i in range(3):
                tile = jnp.where(sub // 2 == i, pltpu.roll(row(field, 4 * q + i, False), (2 * i + 2) % 8, 0), tile)
            up[field * (depth // 4) + q] = tile


def pack_faces(spins, kicks, stiffness):
    _, height, lanes = stiffness.shape
    return pl.pallas_call(
        face_kernel,
        out_shape=[jax.ShapeDtypeStruct((n, height, lanes), F32) for n in (10, 17)],
        in_specs=[pl.BlockSpec(memory_space=pltpu.HBM)] * 3,
        out_specs=[VMEM] * 2,
        scratch_shapes=[pltpu.VMEM((2, 2, height, lanes), F32), pltpu.SemaphoreType.DMA((14,))],
        compiler_params=pltpu.CompilerParams(vmem_limit_bytes=FACE_GRANT),
        cost_estimate=pl.CostEstimate(flops=1_000_000, bytes_accessed=1_000_000, transcendentals=0),
        name="faces",
    )(spins, kicks, stiffness)


def pack_edges(spins, kicks, stiffness, zup, zdn):
    depth, _, lanes = stiffness.shape
    return pl.pallas_call(
        edge_kernel,
        out_shape=[jax.ShapeDtypeStruct((n, 8, lanes), F32) for n in (5 * depth // 4, 5 * depth // 2, CORNERS["end"])],
        in_specs=[pl.BlockSpec(memory_space=pltpu.HBM)] * 3 + [VMEM] * 2,
        out_specs=[VMEM] * 3,
        scratch_shapes=[
            pltpu.VMEM((2, depth, 8, lanes), F32),
            pltpu.VMEM((2, depth, 8, lanes), F32),
            pltpu.VMEM((SWEEPS, 2, depth, 8, lanes), F32),
            pltpu.VMEM((2, depth, 8, lanes), F32),
            pltpu.VMEM((depth, 8, lanes), F32),
            pltpu.VMEM((depth, 8, lanes), F32),
            pltpu.SemaphoreType.DMA((6,)),
        ],
        compiler_params=pltpu.CompilerParams(vmem_limit_bytes=EDGE_GRANT),
        cost_estimate=pl.CostEstimate(flops=1_000_000, bytes_accessed=2_000_000, transcendentals=0),
        name="edges",
    )(spins, kicks, stiffness, zup, zdn)


def small_call(kernel, shapes, *args):
    return pl.pallas_call(
        kernel,
        out_shape=[jax.ShapeDtypeStruct(s, F32) for s in shapes],
        in_specs=[VMEM] * len(args),
        out_specs=[VMEM] * len(shapes),
        compiler_params=pltpu.CompilerParams(vmem_limit_bytes=4 << 20),
        cost_estimate=pl.CostEstimate(flops=100_000, bytes_accessed=1_000_000, transcendentals=0),
    )(*args)


def per_core(moves):
    core = lax.axis_index("gx") % 2
    for c in (0, 1):

        @pl.when(core == c)
        def _():
            for target, at, source, start, count in moves[c]:
                target[at : at + count] = source[start : start + count]


def share_out(lanes, mine, pair):
    def spread(mine, pair, first, second):
        moves = ([], [])
        for core, parts in ((0, (("cdd", 9, first), ("cdu", 9, second))), (1, (("cuu", 5, first), ("cud", 5, second)))):
            for name, count, target in parts:
                moves[core].append((target, 0, mine, CORNERS[name], count))
                moves[core].append((target, 9, pair, CORNERS[name], count))
        per_core(moves)

    return small_call(spread, [(18, 8, lanes)] * 2, mine, pair)


def join(lo, hi):
    def join_edges(lo, hi, out):
        out[: lo.shape[0]] = lo[...]
        out[lo.shape[0] :] = hi[...]

    return small_call(join_edges, [(lo.shape[0] + hi.shape[0], *lo.shape[1:])], lo, hi)[0]


def stack_corners(lanes, first, second):
    def stack(first, second, out):
        out[:18] = first[...]
        out[18:] = second[...]

    return small_call(stack, [(36, 8, lanes)], first, second)[0]


def sort_corners(lanes, got, pair):
    def sort_c(got, pair, own, other):
        moves = ([], [])
        for place, count, start, core in ((0, 5, 0, 1), (5, 5, 18, 1), (10, 9, 18, 0), (19, 9, 0, 0)):
            for c in (0, 1):
                source, flip = (got, 0) if c == core else (pair, 9)
                moves[c].append((own, place, source, start + flip, count))
                moves[c].append((other, place, source, start + 9 - flip, count))
        per_core(moves)

    return small_call(sort_c, [(28, 8, lanes)] * 2, got, pair)


class Rows:
    def __init__(self, S, ST, K, depth, height):
        self.S, self.ST, self.K = S, ST, K
        self.depth, self.height = depth, height
        self.half = height // 2
        self.rows, self.lanes = S.shape[4:]
        lane = lax.broadcasted_iota(jnp.int32, (8, self.lanes), 1)
        self.lane = lane
        self.sub = lax.broadcasted_iota(jnp.int32, (8, self.lanes), 0)
        self.lower8 = self.sub < 4
        self.even = lax.broadcasted_iota(jnp.int32, (self.rows, self.lanes), 1) % 2 == 0
        end = self.lanes - 1
        before = jnp.where(lane == 0, 0, jnp.where(lane == 1, end, lane - 1))
        after = jnp.where(lane == 0, 0, jnp.where(lane == end, 1, lane + 1))
        self.before = jnp.concatenate([before] * (self.rows // 8), axis=0)
        self.after = jnp.concatenate([after] * (self.rows // 8), axis=0)

    def put(self, field, zi, y, x, value):
        if field < 2:
            self.S[field, y, x, zi] = value
        elif field == 2:
            self.ST[y, x, zi] = value
        else:
            self.K[field - 3, y, x, zi] = value

    def edge(self, hi, lo, part, y):
        shift = -(4 * part + 2 * y)
        value = hi if shift == 0 else pltpu.roll(hi, shift % 8, 0)
        shift = (6 - 4 * part) if y == 0 else (4 - 4 * part)
        return jnp.where(self.lower8, value, lo if shift == 0 else pltpu.roll(lo, shift, 0))

    def rows_beyond(self, hi, lo, j, y, second_kick):
        base = 4 * (j % 2)
        if second_kick:
            return pltpu.roll(hi, (-base - 3) % 8, 0) if y == 0 else jnp.zeros(hi.shape, F32)
        above, below = (-base - 2 * y) % 8, 7 - 2 * j - y
        above = pltpu.roll(hi, above, 0) if above else hi
        below = pltpu.roll(lo, below % 8, 0) if below % 8 else lo
        return jnp.where(self.sub < 2 - y, above, jnp.where(self.sub == 7, below, 0.0))

    def place(self, field, zi, body, beyond):
        for y in (0, 1):
            a = jnp.concatenate([body(0, y), beyond(0, y)], axis=0)
            b = jnp.concatenate([body(1, y), beyond(1, y)], axis=0)
            b = pltpu.roll(b, 1, 1)
            self.put(field, zi, y, 0, jnp.where(self.even, a, b))
            self.put(field, zi, y, 1, jnp.where(self.even, b, a))

    def section(self, t, planes):
        S, ST, K = self.S, self.ST, self.K
        sweep, colour = divmod(t, 8)
        yp, xp = (colour // 2) % 2, colour % 2
        acc = jnp.zeros((8, self.lanes), F32)
        for z in planes:
            zi = z + 3
            stiff = ST[yp, xp, zi]
            local = []
            for c in (0, 1):
                along = S[c, yp, 1 - xp, zi]
                if xp == 0:
                    total = jnp.take_along_axis(along, self.before, axis=1) + pltpu.roll(along, self.lanes - 1, 1)
                else:
                    total = jnp.take_along_axis(along, self.after, axis=1) + pltpu.roll(along, 1, 1)
                across = S[c, 1 - yp, xp, zi]
                total = total + (across + pltpu.roll(across, 1 if yp == 0 else self.rows - 1, 0))
                total = total + (S[c, yp, xp, zi - 1] + S[c, yp, xp, zi + 1])
                local.append(stiff * total + K[2 * sweep + c, yp, xp, zi])
            square = local[0] * local[0] + local[1] * local[1]
            scale = lax.rsqrt(1.0 + square)
            for c in (0, 1):
                S[c, yp, xp, zi] = local[c] * scale
            if 0 <= z < self.depth:
                energy = (square * scale)[: self.half]
                acc = acc + sum(energy[8 * j : 8 * j + 8] for j in range(self.half // 8))
        return acc


def inner_planes(depth, t):
    phase = t // 4
    return range(2 + phase, depth - 1 - phase, 2)


def outer_planes(depth, t):
    phase = t // 4
    reach = 2 * (SWEEPS - 1 - t // 8)
    parity = phase % 2
    return [z for z in range(parity - reach, depth - parity + reach + 1, 2) if z not in inner_planes(depth, t)]


def middle_kernel(*refs):
    own, other = refs[:4], refs[4:8]
    S, ST, K, E = refs[8:]
    depth, height, _ = own[2].shape
    rows = Rows(S, ST, K, depth, height)
    sides = (own, other)
    high = 5 * depth // 4

    def four(q, carry):
        for field in ALL:
            source = field if field in FIRST else field - 5
            for j in range(4):
                rows.place(
                    field,
                    4 * q + j + 3,
                    lambda i, y: load_field(*sides[i][:3], field, 4 * q + j, pl.ds(y, height // 2, stride=2)),
                    lambda i, y: rows.rows_beyond(
                        sides[i][3][high + source * (depth // 2) + 2 * q + j // 2],
                        sides[i][3][source * (depth // 4) + q],
                        j,
                        y,
                        field not in FIRST,
                    ),
                )
        return carry

    lax.fori_loop(0, depth // 4, four, 0)
    for t in range(8 * SWEEPS):
        E[t] = rows.section(t, inner_planes(depth, t))


def middle(own, other):
    depth, height, lanes = own[2].shape
    rows = -(-(height // 2 + 4) // 8) * 8
    planes = depth + 7
    return pl.pallas_call(
        middle_kernel,
        out_shape=[
            jax.ShapeDtypeStruct((2, 2, 2, planes, rows, lanes), F32),
            jax.ShapeDtypeStruct((2, 2, planes, rows, lanes), F32),
            jax.ShapeDtypeStruct((2 * SWEEPS, 2, 2, planes, rows, lanes), F32),
            jax.ShapeDtypeStruct((8 * SWEEPS, 8, lanes), F32),
        ],
        in_specs=[VMEM] * 8,
        out_specs=[VMEM] * 4,
        compiler_params=pltpu.CompilerParams(vmem_limit_bytes=8 << 20),
        cost_estimate=pl.CostEstimate(flops=30_000_000, bytes_accessed=10_000_000, transcendentals=0),
        name="middle",
    )(*own, *other)


def last_kernel(*refs):
    E = refs[3]
    own, other = refs[4:7], refs[7:10]
    S, ST, K, out, energies, lines = refs[10:]
    depth, height, lanes = out.shape[1:]
    rows = Rows(S, ST, K, depth, height)
    sides = (own, other)
    for c in range(2):
        for y in range(2):
            for x in range(2):
                S[c, y, x, 0] = jnp.zeros((rows.rows, lanes), F32)
                S[c, y, x, depth + 6] = jnp.zeros((rows.rows, lanes), F32)
    for which, listed, base, lo in ((0, up_planes(depth), -depth, 0), (1, down_planes(), depth, 10)):
        for n, (field, z) in enumerate(listed):
            hi = lo + (5, 9)[which]
            rows.place(
                field,
                z + base + 3,
                lambda i, y: sides[i][which][n, pl.ds(y, height // 2, stride=2), :],
                lambda i, y: rows.edge(sides[i][2][hi + n // 2], sides[i][2][lo + n // 2], n % 2, y),
            )
    for t in range(8 * SWEEPS):
        acc = E[t] + rows.section(t, outer_planes(depth, t))
        mine = rows.lane % 2 == t % 2
        lines[pl.ds(t, 1), :] = jnp.sum(jnp.where(mine, acc, 0.0), axis=0, keepdims=True)

    total = jnp.sum(lines[...], axis=1, keepdims=True)
    diagonal = lax.broadcasted_iota(jnp.int32, lines.shape, 0) == lax.broadcasted_iota(jnp.int32, lines.shape, 1)
    line = jnp.sum(jnp.where(diagonal, total, 0.0), axis=0, keepdims=True)
    energies[...] = jnp.broadcast_to(line, energies.shape)
    half = height // 2

    def write(z, carry):
        for c in (0, 1):
            for y in (0, 1):
                value = jnp.where(rows.even[:half], S[c, y, 0, z + 3, :half], S[c, y, 1, z + 3, :half])
                out[c, z, pl.ds(y, half, stride=2), :] = value
        return carry

    lax.fori_loop(0, depth, write, 0)


def last(state, own, other, shape, devices):
    lanes = shape[-1]
    results = pl.pallas_call(
        last_kernel,
        out_shape=[jax.ShapeDtypeStruct(v.shape, F32) for v in state[:3]]
        + [jax.ShapeDtypeStruct(shape, F32), jax.ShapeDtypeStruct((devices, lanes), F32)],
        in_specs=[VMEM] * 10,
        out_specs=[VMEM] * 5,
        input_output_aliases={0: 0, 1: 1, 2: 2},
        scratch_shapes=[pltpu.VMEM((8 * SWEEPS, lanes), F32)],
        compiler_params=pltpu.CompilerParams(vmem_limit_bytes=8 << 20),
        cost_estimate=pl.CostEstimate(flops=30_000_000, bytes_accessed=10_000_000, transcendentals=0),
        name="last",
    )(*state, *own, *other)
    return results[3:]


def step(spins, kicks, stiffness):
    nz, ny, nx = (lax.axis_size(a) for a in ("gz", "gy", "gx"))
    devices = nz * ny * nx
    sites = jnp.float32(stiffness.size * devices // 8)

    def shift(value, even_core, odd_core):
        pairs = []
        for z in range(nz):
            for y in range(ny):
                for x in range(nx):
                    dz, dy = odd_core if x % 2 else even_core
                    pairs.append(((z * ny + y) * nx + x, ((z + dz) % nz * ny + (y + dy) % ny) * nx + x))
        return lax.ppermute(value, ("gz", "gy", "gx"), pairs)

    def swap(value):
        return lax.ppermute(value, "gx", [(i, i ^ 1) for i in range(nx)])

    lanes = stiffness.shape[-1]

    def beside(value):
        right = lax.ppermute(value, "gx", [((i + 1) % nx, i) for i in range(nx)])
        if nx == 2:
            return right
        left = lax.ppermute(value, "gx", [(i, (i + 1) % nx) for i in range(nx)])
        lane = lax.broadcasted_iota(jnp.int32, value.shape, value.ndim - 1)
        return jnp.where(lane < lanes // 2, right, left)

    raw = (spins, kicks, stiffness)
    zup, zdn = pack_faces(*raw)
    yup, ydn, mine = pack_edges(*raw, zup, zdn)
    first, second = share_out(lanes, mine, swap(mine))
    up, down, left, right = (1, 0), (-1, 0), (0, -1), (0, 1)
    zlo, zhi = shift(zup, up, up), shift(zdn, down, down)
    edges = join(shift(yup, right, right), shift(ydn, left, left))
    corners = stack_corners(lanes, shift(first, (-1, -1), (1, 1)), shift(second, (-1, 1), (1, -1)))
    beyond = beside(edges)
    other = tuple(beside(v) for v in raw)
    state = middle(raw + (edges,), other + (beyond,))
    corners, beyond = sort_corners(lanes, corners, swap(corners))
    if nx > 2:
        beyond = beside(corners)
    other = (beside(zlo), beside(zhi), beyond)
    final, energies = last(state, (zlo, zhi, corners), other, spins.shape, devices)
    parts = lax.all_to_all(energies, ("gz", "gy", "gx"), 0, 0, tiled=True)
    total = jnp.sum(parts, axis=0)[: 8 * SWEEPS]
    return (final, -total / sites)


def solution(mesh):
    placed = (P(None, "gz", "gy", "gx"), P(None, None, "gz", "gy", "gx"), P("gz", "gy", "gx"))
    return jax.shard_map(
        step,
        mesh=mesh,
        in_specs=placed,
        out_specs=(P(None, "gz", "gy", "gx"), P()),
        check_vma=False,
    )
```

profile of v0, /device:TPU:0, one launch (start us, length us, event | category | flops | bytes accessed | tf_op | source)
XLA Modules:
  0.0 51.8 jit_solution(7868072594306243735)
XLA Ops:
  0.6 0.6 %collective-permute-start.3 = (f32[2,2,16,48,128]{4,3,2,1,0:T(8,128)}, f32[2,2,16,48,128]{4,3,2,1,0:T(8,128)S(1)}, u32[]{:S(2)}, u32[]{:S(2)}) collective-permute-start(f32[2,2,16,48,128]{4,3,2,1,0:T(8,128)} %refs_1_.1), channel_id=1, source_target_pairs={{1,0},{0,1},{3,2},{2,3},{5,4},{4,5},{7,6},{6,7},{9,8},{8,9},{11,10... | collective-permute-start | bytes 4718600 | tf_op jit(solution)/shard_map/ppermute | solution.py:443
  1.2 1.1 %copy-done.2 = f32[16,48,128]{2,1,0:T(8,128)S(1)} copy-done((f32[16,48,128]{2,1,0:T(8,128)S(1)}, f32[16,48,128]{2,1,0:T(8,128)}, u32[]{:S(2)}) %copy-start.2) | copy-done | bytes 393240
  2.3 1.3 %faces.1 = (f32[10,48,128]{2,1,0:T(8,128)S(1)}, f32[17,48,128]{2,1,0:T(8,128)S(1)}) custom-call(f32[2,16,48,128]{3,2,1,0:T(8,128)} %refs_0_.1, f32[2,2,16,48,128]{4,3,2,1,0:T(8,128)} %refs_1_.1, f32[16,48,128]{2,1,0:T(8,128)S(1)} %copy-done.2), custom_call_target="tpu_custom_call" | custom-call | flops 1000000 | bytes 1000000 | tf_op jit(solution)/shard_map/faces/pallas_call | solution.py:128
  3.7 0.2 edges.1
  3.9 0.1 collective-permute-start.8
  4.0 4.9 %collective-permute-start.1 = (f32[40,8,128]{2,1,0:T(8,128)S(1)}, f32[40,8,128]{2,1,0:T(8,128)S(1)}, u32[]{:S(2)}, u32[]{:S(2)}) collective-permute-start(f32[40,8,128]{2,1,0:T(8,128)S(1)} %get-tuple-element.20), channel_id=1, source_target_pairs={{0,6},{1,7},{2,0},{3,1},{4,2},{5,3},{6,4},{7,5},{8,14},{9,15},{10,... | collective-permute-start | bytes 491528 | tf_op jit(solution)/shard_map/ppermute | solution.py:435
  8.9 2.4 %collective-permute-start.7 = (f32[17,48,128]{2,1,0:T(8,128)S(1)}, f32[17,48,128]{2,1,0:T(8,128)S(1)}, u32[]{:S(2)}, u32[]{:S(2)}) collective-permute-start(f32[17,48,128]{2,1,0:T(8,128)S(1)} %get-tuple-element.18.zdn), channel_id=1, source_target_pairs={{0,24},{1,25},{2,26},{3,27},{4,28},{5,29},{6,30},{7,31},{8,0},{9,1... | collective-permute-start | bytes 1253384 | tf_op jit(solution)/shard_map/ppermute | solution.py:435
  11.4 0.0 collective-permute-start
  11.4 0.0 collective-permute-done.8.pair
  11.4 0.0 collective-permute-start.2
  11.4 6.2 %collective-permute-done.lo = f32[20,8,128]{2,1,0:T(8,128)S(1)} collective-permute-done((f32[20,8,128]{2,1,0:T(8,128)S(1)}, f32[20,8,128]{2,1,0:T(8,128)S(1)}, u32[]{:S(2)}, u32[]{:S(2)}) %collective-permute-start) | collective-permute-done | bytes 81952 | tf_op jit(solution)/shard_map/ppermute | solution.py:435
  17.6 2.1 %collective-permute-start.9 = (f32[18,8,128]{2,1,0:T(8,128)S(1)}, f32[18,8,128]{2,1,0:T(8,128)S(1)}, u32[]{:S(2)}, u32[]{:S(2)}) collective-permute-start(f32[18,8,128]{2,1,0:T(8,128)S(1)} %get-tuple-element.26), channel_id=1, source_target_pairs={{0,30},{1,11},{2,24},{3,13},{4,26},{5,15},{6,28},{7,9},{8,6},{9,19... | collective-permute-start | bytes 221192 | tf_op jit(solution)/shard_map/ppermute | solution.py:435
  19.7 0.0 collective-permute-done.1.hi
  19.7 0.7 %collective-permute-start.10 = (f32[18,8,128]{2,1,0:T(8,128)S(1)}, f32[18,8,128]{2,1,0:T(8,128)S(1)}, u32[]{:S(2)}, u32[]{:S(2)}) collective-permute-start(f32[18,8,128]{2,1,0:T(8,128)S(1)} %get-tuple-element.27), channel_id=1, source_target_pairs={{0,26},{1,15},{2,28},{3,9},{4,30},{5,11},{6,24},{7,13},{8,2},{9,23... | collective-permute-start | bytes 221192 | tf_op jit(solution)/shard_map/ppermute | solution.py:435
  20.5 3.3 %collective-permute-done.9.first = f32[18,8,128]{2,1,0:T(8,128)S(1)} collective-permute-done((f32[18,8,128]{2,1,0:T(8,128)S(1)}, f32[18,8,128]{2,1,0:T(8,128)S(1)}, u32[]{:S(2)}, u32[]{:S(2)}) %collective-permute-start.9) | collective-permute-done | bytes 73760 | tf_op jit(solution)/shard_map/ppermute | solution.py:435
  23.7 0.6 %collective-permute-start.6 = (f32[10,48,128]{2,1,0:T(8,128)S(1)}, f32[10,48,128]{2,1,0:T(8,128)S(1)}, u32[]{:S(2)}, u32[]{:S(2)}) collective-permute-start(f32[10,48,128]{2,1,0:T(8,128)S(1)} %get-tuple-element.17.zup), channel_id=1, source_target_pairs={{0,8},{1,9},{2,10},{3,11},{4,12},{5,13},{6,14},{7,15},{8,16},{9,17... | collective-permute-start | bytes 737288 | tf_op jit(solution)/shard_map/ppermute | solution.py:435
  24.3 2.6 %collective-permute-done.10.second = f32[18,8,128]{2,1,0:T(8,128)S(1)} collective-permute-done((f32[18,8,128]{2,1,0:T(8,128)S(1)}, f32[18,8,128]{2,1,0:T(8,128)S(1)}, u32[]{:S(2)}, u32[]{:S(2)}) %collective-permute-start.10) | collective-permute-done | bytes 73760 | tf_op jit(solution)/shard_map/ppermute | solution.py:435
  26.9 0.0 collective-permute-start.4
  26.9 0.0 collective-permute-done.7.refs_5_
  26.9 0.5 collective-permute-start.13
  27.4 4.9 %collective-permute-done.6.refs_4_ = f32[10,48,128]{2,1,0:T(8,128)S(1)} collective-permute-done((f32[10,48,128]{2,1,0:T(8,128)S(1)}, f32[10,48,128]{2,1,0:T(8,128)S(1)}, u32[]{:S(2)}, u32[]{:S(2)}) %collective-permute-start.6) | collective-permute-done | bytes 245792 | tf_op jit(solution)/shard_map/ppermute | solution.py:435
  32.4 0.0 collective-permute-start.11
  32.4 1.3 %collective-permute-done.11.pair = f32[36,8,128]{2,1,0:T(8,128)S(1)} collective-permute-done((f32[36,8,128]{2,1,0:T(8,128)S(1)}, f32[36,8,128]{2,1,0:T(8,128)S(1)}, u32[]{:S(2)}, u32[]{:S(2)}) %collective-permute-start.11) | collective-permute-done | bytes 147488 | tf_op jit(solution)/shard_map/ppermute | solution.py:438
  33.7 0.1 collective-permute-start.5
  33.9 0.0 collective-permute-done.4.refs_6_
  33.9 0.4 collective-permute-start.12
  34.3 1.0 %collective-permute-done.5.refs_7_ = f32[60,8,128]{2,1,0:T(8,128)S(1)} collective-permute-done((f32[60,8,128]{2,1,0:T(8,128)S(1)}, f32[60,8,128]{2,1,0:T(8,128)S(1)}, u32[]{:S(2)}, u32[]{:S(2)}) %collective-permute-start.5) | collective-permute-done | bytes 245792 | tf_op jit(solution)/shard_map/ppermute | solution.py:443
  35.3 3.4 %middle.1 = (f32[2,2,2,23,32,128]{5,4,3,2,1,0:T(8,128)S(1)}, f32[2,2,23,32,128]{4,3,2,1,0:T(8,128)S(1)}, f32[4,2,2,23,32,128]{5,4,3,2,1,0:T(8,128)S(1)}, f32[16,8,128]{2,1,0:T(8,128)S(1)}) custom-call(f32[2,16,48,128]{3,2,1,0:T(8,128)S(1)} %copy-done.1, f32[2,2,16,48,128]{4,3,2,1,0:T(8,128)S(1)} %copy-done, f32[16,48,128]{2,1,0:T(8,128)S(1)} %copy-done.2, ...), custom_call_target="tpu_custom_call" | custom-call | flops 30000000 | bytes 10000000 | tf_op jit(solution)/shard_map/middle/pallas_call | solution.py:348
  38.6 3.0 %last.1 = (f32[2,2,2,23,32,128]{5,4,3,2,1,0:T(8,128)S(1)}, f32[2,2,23,32,128]{4,3,2,1,0:T(8,128)S(1)}, f32[4,2,2,23,32,128]{5,4,3,2,1,0:T(8,128)S(1)}, f32[2,16,48,128]{3,2,1,0:T(8,128)}, f32[32,128]{1,0:T(8,128)S(1)}) custom-call(f32[2,2,2,23,32,128]{5,4,3,2,1,0:T(8,128)S(1)} %get-tuple-element.21.refs_0_, ...), custom_call_target="tpu_custom_call", output_to_operand_aliasing={{0}: (0, {}), {1}: (1, {}), {2}: (2, {})} | custom-call | flops 30000000 | bytes 10000000 | tf_op jit(solution)/shard_map/last/pallas_call | solution.py:408
  41.7 9.6 %all_to_all.9 = f32[32,1,128]{2,1,0:T(1,128)S(1)} all-to-all(f32[32,1,128]{2,1,0:T(1,128)S(1)} %bitcast.3), channel_id=1, replica_groups=mesh['gz'=4,'gy'=4,'gx'=2] {'gz','gy','gx'}, dimensions={0} | all-to-all | bytes 32768 | tf_op jit(solution)/shard_map/all_to_all | solution.py:466
  51.3 0.1 reduce_sum.9
  51.3 0.5 negate_multiply_fusion
  (13 shorter events, 0.1 us)
Async XLA Ops:
  0.6 3.0 %copy-start = (f32[2,2,16,48,128]{4,3,2,1,0:T(8,128)S(1)}, f32[2,2,16,48,128]{4,3,2,1,0:T(8,128)}, u32[]{:S(2)}) copy-start(f32[2,2,16,48,128]{4,3,2,1,0:T(8,128)} %refs_1_.1) | copy-start | bytes 4718596
  0.6 3.0 %copy-start.1 = (f32[2,16,48,128]{3,2,1,0:T(8,128)S(1)}, f32[2,16,48,128]{3,2,1,0:T(8,128)}, u32[]{:S(2)}) copy-start(f32[2,16,48,128]{3,2,1,0:T(8,128)} %refs_0_.1) | copy-start | bytes 2359300
  0.6 34.6 %collective-permute-start.3 = (f32[2,2,16,48,128]{4,3,2,1,0:T(8,128)}, f32[2,2,16,48,128]{4,3,2,1,0:T(8,128)S(1)}, u32[]{:S(2)}, u32[]{:S(2)}) collective-permute-start(f32[2,2,16,48,128]{4,3,2,1,0:T(8,128)} %refs_1_.1), channel_id=1, source_target_pairs={{1,0},{0,1},{3,2},{2,3},{5,4},{4,5},{7,6},{6,7},{9,8},{8,9},{11,10... | collective-permute-start | bytes 4718600 | tf_op jit(solution)/shard_map/ppermute | solution.py:443
  1.2 1.1 %copy-start.2 = (f32[16,48,128]{2,1,0:T(8,128)S(1)}, f32[16,48,128]{2,1,0:T(8,128)}, u32[]{:S(2)}) copy-start(f32[16,48,128]{2,1,0:T(8,128)} %refs_2_.1) | copy-start | bytes 1179652
  3.9 7.5 %collective-permute-start.8 = (f32[28,8,128]{2,1,0:T(8,128)S(1)}, f32[28,8,128]{2,1,0:T(8,128)S(1)}, u32[]{:S(2)}, u32[]{:S(2)}) collective-permute-start(f32[28,8,128]{2,1,0:T(8,128)S(1)} %get-tuple-element.25.mine), channel_id=1, source_target_pairs={{0,1},{1,0},{2,3},{3,2},{4,5},{5,4},{6,7},{7,6},{8,9},{9,8},{10,11... | collective-permute-start | bytes 344072 | tf_op jit(solution)/shard_map/ppermute | solution.py:438
  4.0 15.8 %collective-permute-start.1 = (f32[40,8,128]{2,1,0:T(8,128)S(1)}, f32[40,8,128]{2,1,0:T(8,128)S(1)}, u32[]{:S(2)}, u32[]{:S(2)}) collective-permute-start(f32[40,8,128]{2,1,0:T(8,128)S(1)} %get-tuple-element.20), channel_id=1, source_target_pairs={{0,6},{1,7},{2,0},{3,1},{4,2},{5,3},{6,4},{7,5},{8,14},{9,15},{10,... | collective-permute-start | bytes 491528 | tf_op jit(solution)/shard_map/ppermute | solution.py:435
  8.9 18.0 %collective-permute-start.7 = (f32[17,48,128]{2,1,0:T(8,128)S(1)}, f32[17,48,128]{2,1,0:T(8,128)S(1)}, u32[]{:S(2)}, u32[]{:S(2)}) collective-permute-start(f32[17,48,128]{2,1,0:T(8,128)S(1)} %get-tuple-element.18.zdn), channel_id=1, source_target_pairs={{0,24},{1,25},{2,26},{3,27},{4,28},{5,29},{6,30},{7,31},{8,0},{9,1... | collective-permute-start | bytes 1253384 | tf_op jit(solution)/shard_map/ppermute | solution.py:435
  11.4 6.2 %collective-permute-start = (f32[20,8,128]{2,1,0:T(8,128)S(1)}, f32[20,8,128]{2,1,0:T(8,128)S(1)}, u32[]{:S(2)}, u32[]{:S(2)}) collective-permute-start(f32[20,8,128]{2,1,0:T(8,128)S(1)} %get-tuple-element.19), channel_id=1, source_target_pairs={{0,2},{1,3},{2,4},{3,5},{4,6},{5,7},{6,0},{7,1},{8,10},{9,11},{10,... | collective-permute-start | bytes 245768 | tf_op jit(solution)/shard_map/ppermute | solution.py:435
  11.4 23.9 %collective-permute-start.2 = (f32[2,16,48,128]{3,2,1,0:T(8,128)S(1)}, f32[2,16,48,128]{3,2,1,0:T(8,128)S(1)}, u32[]{:S(2)}, u32[]{:S(2)}) collective-permute-start(f32[2,16,48,128]{3,2,1,0:T(8,128)S(1)} %copy-done.1), channel_id=1, source_target_pairs={{1,0},{0,1},{3,2},{2,3},{5,4},{4,5},{7,6},{6,7},{9,8},{8,9},{11,10... | collective-permute-start | bytes 2359304 | tf_op jit(solution)/shard_map/ppermute | solution.py:443
  17.6 6.1 %collective-permute-start.9 = (f32[18,8,128]{2,1,0:T(8,128)S(1)}, f32[18,8,128]{2,1,0:T(8,128)S(1)}, u32[]{:S(2)}, u32[]{:S(2)}) collective-permute-start(f32[18,8,128]{2,1,0:T(8,128)S(1)} %get-tuple-element.26), channel_id=1, source_target_pairs={{0,30},{1,11},{2,24},{3,13},{4,26},{5,15},{6,28},{7,9},{8,6},{9,19... | collective-permute-start | bytes 221192 | tf_op jit(solution)/shard_map/ppermute | solution.py:435
  19.7 7.2 %collective-permute-start.10 = (f32[18,8,128]{2,1,0:T(8,128)S(1)}, f32[18,8,128]{2,1,0:T(8,128)S(1)}, u32[]{:S(2)}, u32[]{:S(2)}) collective-permute-start(f32[18,8,128]{2,1,0:T(8,128)S(1)} %get-tuple-element.27), channel_id=1, source_target_pairs={{0,26},{1,15},{2,28},{3,9},{4,30},{5,11},{6,24},{7,13},{8,2},{9,23... | collective-permute-start | bytes 221192 | tf_op jit(solution)/shard_map/ppermute | solution.py:435
  23.7 8.6 %collective-permute-start.6 = (f32[10,48,128]{2,1,0:T(8,128)S(1)}, f32[10,48,128]{2,1,0:T(8,128)S(1)}, u32[]{:S(2)}, u32[]{:S(2)}) collective-permute-start(f32[10,48,128]{2,1,0:T(8,128)S(1)} %get-tuple-element.17.zup), channel_id=1, source_target_pairs={{0,8},{1,9},{2,10},{3,11},{4,12},{5,13},{6,14},{7,15},{8,16},{9,17... | collective-permute-start | bytes 737288 | tf_op jit(solution)/shard_map/ppermute | solution.py:435
  26.9 7.0 %collective-permute-start.4 = (f32[16,48,128]{2,1,0:T(8,128)S(1)}, f32[16,48,128]{2,1,0:T(8,128)S(1)}, u32[]{:S(2)}, u32[]{:S(2)}) collective-permute-start(f32[16,48,128]{2,1,0:T(8,128)S(1)} %copy-done.2), channel_id=1, source_target_pairs={{1,0},{0,1},{3,2},{2,3},{5,4},{4,5},{7,6},{6,7},{9,8},{8,9},{11,10... | collective-permute-start | bytes 1179656 | tf_op jit(solution)/shard_map/ppermute | solution.py:443
  26.9 11.7 %collective-permute-start.13 = (f32[17,48,128]{2,1,0:T(8,128)S(1)}, f32[17,48,128]{2,1,0:T(8,128)S(1)}, u32[]{:S(2)}, u32[]{:S(2)}) collective-permute-start(f32[17,48,128]{2,1,0:T(8,128)S(1)} %collective-permute-done.7.refs_5_), channel_id=1, source_target_pairs={{1,0},{0,1},{3,2},{2,3},{5,4},{4,5},{7,6},{6,7},{9,8},{8,9},{11,10... | collective-permute-start | bytes 1253384 | tf_op jit(solution)/shard_map/ppermute | solution.py:443
  32.4 1.4 %collective-permute-start.11 = (f32[36,8,128]{2,1,0:T(8,128)S(1)}, f32[36,8,128]{2,1,0:T(8,128)S(1)}, u32[]{:S(2)}, u32[]{:S(2)}) collective-permute-start(f32[36,8,128]{2,1,0:T(8,128)S(1)} %shard_map.52.got), channel_id=1, source_target_pairs={{0,1},{1,0},{2,3},{3,2},{4,5},{5,4},{6,7},{7,6},{8,9},{9,8},{10,11... | collective-permute-start | bytes 442376 | tf_op jit(solution)/shard_map/ppermute | solution.py:438
  33.7 1.5 %collective-permute-start.5 = (f32[60,8,128]{2,1,0:T(8,128)S(1)}, f32[60,8,128]{2,1,0:T(8,128)S(1)}, u32[]{:S(2)}, u32[]{:S(2)}) collective-permute-start(f32[60,8,128]{2,1,0:T(8,128)S(1)} %shard_map.50.refs_3_), channel_id=1, source_target_pairs={{1,0},{0,1},{3,2},{2,3},{5,4},{4,5},{7,6},{6,7},{9,8},{8,9},{11,10... | collective-permute-start | bytes 737288 | tf_op jit(solution)/shard_map/ppermute | solution.py:443
  33.9 4.7 %collective-permute-start.12 = (f32[10,48,128]{2,1,0:T(8,128)S(1)}, f32[10,48,128]{2,1,0:T(8,128)S(1)}, u32[]{:S(2)}, u32[]{:S(2)}) collective-permute-start(f32[10,48,128]{2,1,0:T(8,128)S(1)} %collective-permute-done.6.refs_4_), channel_id=1, source_target_pairs={{1,0},{0,1},{3,2},{2,3},{5,4},{4,5},{7,6},{6,7},{9,8},{8,9},{11,10... | collective-permute-start | bytes 737288 | tf_op jit(solution)/shard_map/ppermute | solution.py:443
where the time goes:
time: 52 us; the launch traced here: 51.8 us
  waiting for transfers between devices  19.3 us (37%)
  starting transfers between devices  12.5 us (24%)
  blocking collectives  9.58 us (18%)
  Pallas kernels  7.98 us (15%)
  local copies, waits for them, and re-layouts  1.14 us (2%)
  between operations  0.74 us (1%)
  other arithmetic  0.57 us (1%)
    ppermute x6, waiting for transfers between devices, shift(): return lax.ppermute(value, ('gz', 'gy', 'gx'), pairs)  17 us
    ppermute x6, starting transfers between devices, shift(): return lax.ppermute(value, ('gz', 'gy', 'gx'), pairs)  10.8 us
    all_to_all x1, blocking collectives, step(): parts = lax.all_to_all(energies, ('gz', 'gy', 'gx'), 0, 0, tiled=True)  9.58 us
    pallas_call x1, Pallas kernels, middle(): pl.pallas_call(middle_kernel, out_shape=[jax.ShapeDtypeStruct((2, 2, 2, p...  3.35 us
    pallas_call x1, Pallas kernels, last(): pl.pallas_call(last_kernel, out_shape=[jax.ShapeDtypeStruct(v.shape, F32)...  3.04 us
    ppermute x6, starting transfers between devices, beside(): right = lax.ppermute(value, 'gx', [((i + 1) % nx, i) for i in range(nx)])  1.58 us
    ppermute x2, waiting for transfers between devices, swap(): return lax.ppermute(value, 'gx', [(i, i ^ 1) for i in range(nx)])  1.35 us
    pallas_call x1, Pallas kernels, pack_faces(): pl.pallas_call(face_kernel, out_shape=[jax.ShapeDtypeStruct((n, height, l...  1.29 us
  transfers between devices with their start and end apart: 14, of which 6 were waited for; matrix products, arithmetic and copies ran while one was open for 0% of the time, Pallas kernels for 10%

commit v1 on v0

--- a/solution.py
+++ b/solution.py
@@ -238,13 +238,18 @@
         self.before = jnp.concatenate([before] * (self.rows // 8), axis=0)
         self.after = jnp.concatenate([after] * (self.rows // 8), axis=0)
 
-    def put(self, field, zi, y, x, value):
-        if field < 2:
-            self.S[field, y, x, zi] = value
-        elif field == 2:
-            self.ST[y, x, zi] = value
-        else:
-            self.K[field - 3, y, x, zi] = value
+    def put(self, field, zi, y, start, a, b):
+        b = pltpu.roll(b, 1, 1)
+        even = self.even[: a.shape[0]]
+        for x in (0, 1):
+            value = jnp.where(even, a, b) if x == 0 else jnp.where(even, b, a)
+            at = (y, x, zi, pl.ds(start, a.shape[0]))
+            if field < 2:
+                self.S[(field, *at)] = value
+            elif field == 2:
+                self.ST[at] = value
+            else:
+                self.K[(field - 3, *at)] = value
 
     def edge(self, hi, lo, part, y):
         shift = -(4 * part + 2 * y)
@@ -260,14 +265,6 @@
         above = pltpu.roll(hi, above, 0) if above else hi
         below = pltpu.roll(lo, below % 8, 0) if below % 8 else lo
         return jnp.where(self.sub < 2 - y, above, jnp.where(self.sub == 7, below, 0.0))
-
-    def place(self, field, zi, body, beyond):
-        for y in (0, 1):
-            a = jnp.concatenate([body(0, y), beyond(0, y)], axis=0)
-            b = jnp.concatenate([body(1, y), beyond(1, y)], axis=0)
-            b = pltpu.roll(b, 1, 1)
-            self.put(field, zi, y, 0, jnp.where(self.even, a, b))
-            self.put(field, zi, y, 1, jnp.where(self.even, b, a))
 
     def section(self, t, planes):
         S, ST, K = self.S, self.ST, self.K
@@ -310,30 +307,66 @@
     return [z for z in range(parity - reach, depth - parity + reach + 1, 2) if z not in inner_planes(depth, t)]
 
 
-def middle_kernel(*refs):
-    own, other = refs[:4], refs[4:8]
-    S, ST, K, E = refs[8:]
+def build_kernel(*refs):
+    own, other = refs[:3], refs[3:6]
+    S, ST, K = refs[6:]
     depth, height, _ = own[2].shape
     rows = Rows(S, ST, K, depth, height)
-    sides = (own, other)
+
+    def two(p, carry):
+        for field in ALL:
+            for z in (2 * p, 2 * p + 1):
+                for y in (0, 1):
+                    a, b = (load_field(*side, field, z, pl.ds(y, height // 2, stride=2)) for side in (own, other))
+                    rows.put(field, z + 3, y, 0, a, b)
+        return carry
+
+    lax.fori_loop(0, depth // 2, two, 0)
+
+
+def build(own, other):
+    depth, height, lanes = own[2].shape
+    rows = -(-(height // 2 + 4) // 8) * 8
+    planes = depth + 7
+    return pl.pallas_call(
+        build_kernel,
+        out_shape=[
+            jax.ShapeDtypeStruct((2, 2, 2, planes, rows, lanes), F32),
+            jax.ShapeDtypeStruct((2, 2, planes, rows, lanes), F32),
+            jax.ShapeDtypeStruct((2 * SWEEPS, 2, 2, planes, rows, lanes), F32),
+        ],
+        in_specs=[VMEM] * 6,
+        out_specs=[VMEM] * 3,
+        compiler_params=pltpu.CompilerParams(vmem_limit_bytes=8 << 20),
+        cost_estimate=pl.CostEstimate(flops=30_000_000, bytes_accessed=10_000_000, transcendentals=0),
+        name="build",
+    )(*own, *other)
+
+
+def middle_kernel(*refs):
+    sides = refs[3:5]
+    height = 2 * refs[5][0]
+    S, ST, K, E = refs[6:]
+    depth = S.shape[3] - 7
+    rows = Rows(S, ST, K, depth, height)
     high = 5 * depth // 4
 
     def four(q, carry):
         for field in ALL:
             source = field if field in FIRST else field - 5
             for j in range(4):
-                rows.place(
-                    field,
-                    4 * q + j + 3,
-                    lambda i, y: load_field(*sides[i][:3], field, 4 * q + j, pl.ds(y, height // 2, stride=2)),
-                    lambda i, y: rows.rows_beyond(
-                        sides[i][3][high + source * (depth // 2) + 2 * q + j // 2],
-                        sides[i][3][source * (depth // 4) + q],
-                        j,
-                        y,
-                        field not in FIRST,
-                    ),
-                )
+                for y in (0, 1):
+                    a, b = (
+                        rows.rows_beyond(
+                            side[high + source * (depth // 2) + 2 * q + j // 2],
+                            side[source * (depth // 4) + q],
+                            j,
+                            y,
+                            field not in FIRST,
+                        )
+                        for side in sides
+                    )
+                    rows.put(field, 4 * q + j + 3, y, height // 2, a, b)
         return carry
 
     lax.fori_loop(0, depth // 4, four, 0)
@@ -341,30 +374,28 @@
         E[t] = rows.section(t, inner_planes(depth, t))
 
 
-def middle(own, other):
-    depth, height, lanes = own[2].shape
-    rows = -(-(height // 2 + 4) // 8) * 8
-    planes = depth + 7
+def middle(state, own, other, height):
+    lanes = own.shape[-1]
+
+    def kernel(*refs):
+        middle_kernel(*refs[:5], (height // 2,), *refs[5:])
+
     return pl.pallas_call(
-        middle_kernel,
-        out_shape=[
-            jax.ShapeDtypeStruct((2, 2, 2, planes, rows, lanes), F32),
-            jax.ShapeDtypeStruct((2, 2, planes, rows, lanes), F32),
-            jax.ShapeDtypeStruct((2 * SWEEPS, 2, 2, planes, rows, lanes), F32),
-            jax.ShapeDtypeStruct((8 * SWEEPS, 8, lanes), F32),
-        ],
-        in_specs=[VMEM] * 8,
+        kernel,
+        out_shape=[jax.ShapeDtypeStruct(v.shape, F32) for v in state] + [jax.ShapeDtypeStruct((8 * SWEEPS, 8, lanes), F32)],
+        in_specs=[VMEM] * 5,
         out_specs=[VMEM] * 4,
+        input_output_aliases={0: 0, 1: 1, 2: 2},
         compiler_params=pltpu.CompilerParams(vmem_limit_bytes=8 << 20),
         cost_estimate=pl.CostEstimate(flops=30_000_000, bytes_accessed=10_000_000, transcendentals=0),
         name="middle",
-    )(*own, *other)
+    )(*state, own, other)
 
 
 def last_kernel(*refs):
     E = refs[3]
     own, other = refs[4:7], refs[7:10]
-    S, ST, K, out, energies, lines = refs[10:]
+    S, ST, K, out, energies, lines, final, sems = refs[10:]
     depth, height, lanes = out.shape[1:]
     rows = Rows(S, ST, K, depth, height)
     sides = (own, other)
@@ -376,31 +407,47 @@
     for which, listed, base, lo in ((0, up_planes(depth), -depth, 0), (1, down_planes(), depth, 10)):
         for n, (field, z) in enumerate(listed):
             hi = lo + (5, 9)[which]
-            rows.place(
-                field,
-                z + base + 3,
-                lambda i, y: sides[i][which][n, pl.ds(y, height // 2, stride=2), :],
-                lambda i, y: rows.edge(sides[i][2][hi + n // 2], sides[i][2][lo + n // 2], n % 2, y),
-            )
+            for y in (0, 1):
+                a, b = (
+                    jnp.concatenate(
+                        [
+                            side[which][n, pl.ds(y, height // 2, stride=2), :],
+                            rows.edge(side[2][hi + n // 2], side[2][lo + n // 2], n % 2, y),
+                        ],
+                        axis=0,
+                    )
+                    for side in sides
+                )
+                rows.put(field, z + base + 3, y, 0, a, b)
+    half = height // 2
+    sent = []
+
+    def send(start, stop):
+        for z in range(start, stop):
+            for c in (0, 1):
+                for y in (0, 1):
+                    value = jnp.where(rows.even[:half], S[c, y, 0, z + 3, :half], S[c, y, 1, z + 3, :half])
+                    final[c, z, pl.ds(y, half, stride=2), :] = value
+        part = pl.ds(start, stop - start)
+        copy = pltpu.make_async_copy(final.at[:, part], out.at[:, part], sems.at[len(sent)])
+        copy.start()
+        sent.append(copy)
+
+    low, high = 2 * SWEEPS, depth - 2 * SWEEPS + 1
+    send(low, high)
     for t in range(8 * SWEEPS):
         acc = E[t] + rows.section(t, outer_planes(depth, t))
         mine = rows.lane % 2 == t % 2
         lines[pl.ds(t, 1), :] = jnp.sum(jnp.where(mine, acc, 0.0), axis=0, keepdims=True)
 
+    send(0, low)
+    send(high, depth)
     total = jnp.sum(lines[...], axis=1, keepdims=True)
     diagonal = lax.broadcasted_iota(jnp.int32, lines.shape, 0) == lax.broadcasted_iota(jnp.int32, lines.shape, 1)
     line = jnp.sum(jnp.where(diagonal, total, 0.0), axis=0, keepdims=True)
     energies[...] = jnp.broadcast_to(line, energies.shape)
-    half = height // 2
-
-    def write(z, carry):
-        for c in (0, 1):
-            for y in (0, 1):
-                value = jnp.where(rows.even[:half], S[c, y, 0, z + 3, :half], S[c, y, 1, z + 3, :half])
-                out[c, z, pl.ds(y, half, stride=2), :] = value
-        return carry
-
-    lax.fori_loop(0, depth, write, 0)
+    for copy in sent:
+        copy.wait()
 
 
 def last(state, own, other, shape, devices):
@@ -410,9 +457,13 @@
         out_shape=[jax.ShapeDtypeStruct(v.shape, F32) for v in state[:3]]
         + [jax.ShapeDtypeStruct(shape, F32), jax.ShapeDtypeStruct((devices, lanes), F32)],
         in_specs=[VMEM] * 10,
-        out_specs=[VMEM] * 5,
+        out_specs=[VMEM] * 3 + [pl.BlockSpec(memory_space=pltpu.HBM), VMEM],
         input_output_aliases={0: 0, 1: 1, 2: 2},
-        scratch_shapes=[pltpu.VMEM((8 * SWEEPS, lanes), F32)],
+        scratch_shapes=[
+            pltpu.VMEM((8 * SWEEPS, lanes), F32),
+            pltpu.VMEM(shape, F32),
+            pltpu.SemaphoreType.DMA((3,)),
+        ],
         compiler_params=pltpu.CompilerParams(vmem_limit_bytes=8 << 20),
         cost_estimate=pl.CostEstimate(flops=30_000_000, bytes_accessed=10_000_000, transcendentals=0),
         name="last",
@@ -457,7 +508,8 @@
     corners = stack_corners(lanes, shift(first, (-1, -1), (1, 1)), shift(second, (-1, 1), (1, -1)))
     beyond = beside(edges)
     other = tuple(beside(v) for v in raw)
-    state = middle(raw + (edges,), other + (beyond,))
+    state = build(raw, other)
+    state = middle(state, edges, beyond, stiffness.shape[1])
     corners, beyond = sort_corners(lanes, corners, swap(corners))
     if nx > 2:
         beyond = beside(corners)

time: 52 us -> 51.3 us (0.987)
  waiting for transfers between devices: 19.3 us -> 18.3 us
    ppermute x6, waiting for transfers between devices: 0.99 us -> 0.02 us  [beside(): right = lax.ppermute(value, 'gx', [((i + 1) % nx, i) for i in range(nx)])]
    pallas_call x1 -> x2, Pallas kernels: 3.35 us -> 3.92 us  [the longest x1 2.67 us: middle(): pl.pallas_call(kernel, out_shape=[jax.ShapeDtypeStruct(v.shape, F32) for...]
  transfers between devices with their start and end apart: 14 -> 14, of which waited for: 6 -> 5; matrix products, arithmetic and copies ran while one was open for 0% -> 0% of each run, Pallas kernels for 10% -> 11%
where the time goes in v1:
time: 51.3 us; the launch traced here: 51.1 us
  waiting for transfers between devices  18.3 us (36%)
  starting transfers between devices  12.5 us (24%)
  blocking collectives  9.59 us (19%)
  Pallas kernels  8.18 us (16%)
  local copies, waits for them, and re-layouts  1.14 us (2%)
  between operations  0.78 us (2%)
  other arithmetic  0.57 us (1%)
    ppermute x6, waiting for transfers between devices, shift(): return lax.ppermute(value, ('gz', 'gy', 'gx'), pairs)  17 us
    ppermute x6, starting transfers between devices, shift(): return lax.ppermute(value, ('gz', 'gy', 'gx'), pairs)  10.8 us
    all_to_all x1, blocking collectives, step(): parts = lax.all_to_all(energies, ('gz', 'gy', 'gx'), 0, 0, tiled=True)  9.59 us
    pallas_call x1, Pallas kernels, middle(): pl.pallas_call(kernel, out_shape=[jax.ShapeDtypeStruct(v.shape, F32) for...  2.67 us
    pallas_call x1, Pallas kernels, last(): pl.pallas_call(last_kernel, out_shape=[jax.ShapeDtypeStruct(v.shape, F32)...  2.67 us
    ppermute x6, starting transfers between devices, beside(): right = lax.ppermute(value, 'gx', [((i + 1) % nx, i) for i in range(nx)])  1.58 us
    ppermute x2, waiting for transfers between devices, swap(): return lax.ppermute(value, 'gx', [(i, i ^ 1) for i in range(nx)])  1.35 us
    pallas_call x1, Pallas kernels, pack_faces(): pl.pallas_call(face_kernel, out_shape=[jax.ShapeDtypeStruct((n, height, l...  1.29 us
  transfers between devices with their start and end apart: 14, of which 5 were waited for; matrix products, arithmetic and copies ran while one was open for 0% of the time, Pallas kernels for 11%

profile of v1, /device:TPU:0, one launch (start us, length us, event | category | flops | bytes accessed | tf_op | source)
XLA Modules:
  0.0 51.1 jit_solution(11136363228092392146)
XLA Ops:
  0.6 0.6 %collective-permute-start.1 = (f32[2,2,16,48,128]{4,3,2,1,0:T(8,128)}, f32[2,2,16,48,128]{4,3,2,1,0:T(8,128)S(1)}, u32[]{:S(2)}, u32[]{:S(2)}) collective-permute-start(f32[2,2,16,48,128]{4,3,2,1,0:T(8,128)} %k_ref.3), channel_id=1, source_target_pairs={{1,0},{0,1},{3,2},{2,3},{5,4},{4,5},{7,6},{6,7},{9,8},{8,9},{11,10... | collective-permute-start | bytes 4718600 | tf_op jit(solution)/shard_map/ppermute | solution.py:494
  1.2 1.1 %copy-done.2 = f32[16,48,128]{2,1,0:T(8,128)S(1)} copy-done((f32[16,48,128]{2,1,0:T(8,128)S(1)}, f32[16,48,128]{2,1,0:T(8,128)}, u32[]{:S(2)}) %copy-start.2) | copy-done | bytes 393240
  2.3 1.3 %faces.1 = (f32[10,48,128]{2,1,0:T(8,128)S(1)}, f32[17,48,128]{2,1,0:T(8,128)S(1)}) custom-call(f32[2,16,48,128]{3,2,1,0:T(8,128)} %s_ref.3, f32[2,2,16,48,128]{4,3,2,1,0:T(8,128)} %k_ref.3, f32[16,48,128]{2,1,0:T(8,128)S(1)} %copy-done.2), custom_call_target="tpu_custom_call" | custom-call | flops 1000000 | bytes 1000000 | tf_op jit(solution)/shard_map/faces/pallas_call | solution.py:128
  3.7 0.2 edges.1
  3.9 0.1 collective-permute-start.8
  4.0 4.9 %collective-permute-start.4 = (f32[40,8,128]{2,1,0:T(8,128)S(1)}, f32[40,8,128]{2,1,0:T(8,128)S(1)}, u32[]{:S(2)}, u32[]{:S(2)}) collective-permute-start(f32[40,8,128]{2,1,0:T(8,128)S(1)} %get-tuple-element.26), channel_id=1, source_target_pairs={{0,6},{1,7},{2,0},{3,1},{4,2},{5,3},{6,4},{7,5},{8,14},{9,15},{10,... | collective-permute-start | bytes 491528 | tf_op jit(solution)/shard_map/ppermute | solution.py:486
  8.9 2.4 %collective-permute-start.7 = (f32[17,48,128]{2,1,0:T(8,128)S(1)}, f32[17,48,128]{2,1,0:T(8,128)S(1)}, u32[]{:S(2)}, u32[]{:S(2)}) collective-permute-start(f32[17,48,128]{2,1,0:T(8,128)S(1)} %get-tuple-element.24.zdn), channel_id=1, source_target_pairs={{0,24},{1,25},{2,26},{3,27},{4,28},{5,29},{6,30},{7,31},{8,0},{9,1... | collective-permute-start | bytes 1253384 | tf_op jit(solution)/shard_map/ppermute | solution.py:486
  11.4 0.0 collective-permute-start.3
  11.4 0.0 collective-permute-done.8.pair
  11.4 6.2 %collective-permute-done.3.lo = f32[20,8,128]{2,1,0:T(8,128)S(1)} collective-permute-done((f32[20,8,128]{2,1,0:T(8,128)S(1)}, f32[20,8,128]{2,1,0:T(8,128)S(1)}, u32[]{:S(2)}, u32[]{:S(2)}) %collective-permute-start.3) | collective-permute-done | bytes 81952 | tf_op jit(solution)/shard_map/ppermute | solution.py:486
  17.6 2.1 %collective-permute-start.9 = (f32[18,8,128]{2,1,0:T(8,128)S(1)}, f32[18,8,128]{2,1,0:T(8,128)S(1)}, u32[]{:S(2)}, u32[]{:S(2)}) collective-permute-start(f32[18,8,128]{2,1,0:T(8,128)S(1)} %get-tuple-element.32), channel_id=1, source_target_pairs={{0,30},{1,11},{2,24},{3,13},{4,26},{5,15},{6,28},{7,9},{8,6},{9,19... | collective-permute-start | bytes 221192 | tf_op jit(solution)/shard_map/ppermute | solution.py:486
  19.7 0.0 collective-permute-done.4.hi
  19.7 0.7 %collective-permute-start.10 = (f32[18,8,128]{2,1,0:T(8,128)S(1)}, f32[18,8,128]{2,1,0:T(8,128)S(1)}, u32[]{:S(2)}, u32[]{:S(2)}) collective-permute-start(f32[18,8,128]{2,1,0:T(8,128)S(1)} %get-tuple-element.33), channel_id=1, source_target_pairs={{0,26},{1,15},{2,28},{3,9},{4,30},{5,11},{6,24},{7,13},{8,2},{9,23... | collective-permute-start | bytes 221192 | tf_op jit(solution)/shard_map/ppermute | solution.py:486
  20.5 3.3 %collective-permute-done.9.first = f32[18,8,128]{2,1,0:T(8,128)S(1)} collective-permute-done((f32[18,8,128]{2,1,0:T(8,128)S(1)}, f32[18,8,128]{2,1,0:T(8,128)S(1)}, u32[]{:S(2)}, u32[]{:S(2)}) %collective-permute-start.9) | collective-permute-done | bytes 73760 | tf_op jit(solution)/shard_map/ppermute | solution.py:486
  23.7 0.6 %collective-permute-start.6 = (f32[10,48,128]{2,1,0:T(8,128)S(1)}, f32[10,48,128]{2,1,0:T(8,128)S(1)}, u32[]{:S(2)}, u32[]{:S(2)}) collective-permute-start(f32[10,48,128]{2,1,0:T(8,128)S(1)} %get-tuple-element.23.zup), channel_id=1, source_target_pairs={{0,8},{1,9},{2,10},{3,11},{4,12},{5,13},{6,14},{7,15},{8,16},{9,17... | collective-permute-start | bytes 737288 | tf_op jit(solution)/shard_map/ppermute | solution.py:486
  24.3 2.6 %collective-permute-done.10.second = f32[18,8,128]{2,1,0:T(8,128)S(1)} collective-permute-done((f32[18,8,128]{2,1,0:T(8,128)S(1)}, f32[18,8,128]{2,1,0:T(8,128)S(1)}, u32[]{:S(2)}, u32[]{:S(2)}) %collective-permute-start.10) | collective-permute-done | bytes 73760 | tf_op jit(solution)/shard_map/ppermute | solution.py:486
  26.9 0.0 collective-permute-start.2
  26.9 0.5 collective-permute-start.13
  27.4 4.9 %collective-permute-done.6.refs_4_ = f32[10,48,128]{2,1,0:T(8,128)S(1)} collective-permute-done((f32[10,48,128]{2,1,0:T(8,128)S(1)}, f32[10,48,128]{2,1,0:T(8,128)S(1)}, u32[]{:S(2)}, u32[]{:S(2)}) %collective-permute-start.6) | collective-permute-done | bytes 245792 | tf_op jit(solution)/shard_map/ppermute | solution.py:486
  32.4 1.3 %collective-permute-done.11.pair = f32[36,8,128]{2,1,0:T(8,128)S(1)} collective-permute-done((f32[36,8,128]{2,1,0:T(8,128)S(1)}, f32[36,8,128]{2,1,0:T(8,128)S(1)}, u32[]{:S(2)}, u32[]{:S(2)}) %collective-permute-start.11) | collective-permute-done | bytes 147488 | tf_op jit(solution)/shard_map/ppermute | solution.py:489
  33.7 0.1 collective-permute-start.5
  33.9 0.0 collective-permute-done.2.refs_5_
  33.9 0.4 collective-permute-start.12
  34.3 0.0 collective-permute-done.refs_3_
  34.3 1.2 %build.1 = (f32[2,2,2,23,32,128]{5,4,3,2,1,0:T(8,128)S(1)}, f32[2,2,23,32,128]{4,3,2,1,0:T(8,128)S(1)}, f32[4,2,2,23,32,128]{5,4,3,2,1,0:T(8,128)S(1)}) custom-call(f32[2,16,48,128]{3,2,1,0:T(8,128)S(1)} %copy-done.1, f32[2,2,16,48,128]{4,3,2,1,0:T(8,128)S(1)} %copy-done, f32[16,48,128]{2,1,0:T(8,128)S(1)} %copy-done.2, ...), custom_call_target="tpu_custom_call" | custom-call | flops 30000000 | bytes 10000000 | tf_op jit(solution)/shard_map/build/pallas_call | solution.py:331
  35.6 0.0 collective-permute-done.5.refs_4_
  35.6 2.7 %middle.1 = (f32[2,2,2,23,32,128]{5,4,3,2,1,0:T(8,128)S(1)}, f32[2,2,23,32,128]{4,3,2,1,0:T(8,128)S(1)}, f32[4,2,2,23,32,128]{5,4,3,2,1,0:T(8,128)S(1)}, f32[16,8,128]{2,1,0:T(8,128)S(1)}) custom-call(f32[2,2,2,23,32,128]{5,4,3,2,1,0:T(8,128)S(1)} %get-tuple-element.20.refs_0_, ...), custom_call_target="tpu_custom_call", output_to_operand_aliasing={{0}: (0, {}), {1}: (1, {}), {2}: (2, {})} | custom-call | flops 30000000 | bytes 10000000 | tf_op jit(solution)/shard_map/middle/pallas_call | solution.py:383
  38.2 0.0 collective-permute-done.12.refs_7_
  38.3 2.7 %last.1 = (f32[2,2,2,23,32,128]{5,4,3,2,1,0:T(8,128)S(1)}, f32[2,2,23,32,128]{4,3,2,1,0:T(8,128)S(1)}, f32[4,2,2,23,32,128]{5,4,3,2,1,0:T(8,128)S(1)}, f32[2,16,48,128]{3,2,1,0:T(8,128)}, f32[32,128]{1,0:T(8,128)S(1)}) custom-call(f32[2,2,2,23,32,128]{5,4,3,2,1,0:T(8,128)S(1)} %get-tuple-element.27.refs_0_, ...), custom_call_target="tpu_custom_call", output_to_operand_aliasing={{0}: (0, {}), {1}: (1, {}), {2}: (2, {})} | custom-call | flops 30000000 | bytes 10000000 | tf_op jit(solution)/shard_map/last/pallas_call | solution.py:455
  40.9 9.6 %all_to_all.9 = f32[32,1,128]{2,1,0:T(1,128)S(1)} all-to-all(f32[32,1,128]{2,1,0:T(1,128)S(1)} %bitcast.3), channel_id=1, replica_groups=mesh['gz'=4,'gy'=4,'gx'=2] {'gz','gy','gx'}, dimensions={0} | all-to-all | bytes 32768 | tf_op jit(solution)/shard_map/all_to_all | solution.py:518
  50.5 0.1 reduce_sum.9
  50.6 0.5 %negate_multiply_fusion = f32[16]{0:T(128)} fusion(f32[128]{0:T(128)S(1)} %reduce_sum.9), kind=kLoop, calls=%fused_computation | loop fusion | flops 32 | bytes 128 | tf_op jit(solution)/shard_map/div | solution.py:520
  (14 shorter events, 0.1 us)
Async XLA Ops:
  0.6 3.0 %copy-start = (f32[2,2,16,48,128]{4,3,2,1,0:T(8,128)S(1)}, f32[2,2,16,48,128]{4,3,2,1,0:T(8,128)}, u32[]{:S(2)}) copy-start(f32[2,2,16,48,128]{4,3,2,1,0:T(8,128)} %k_ref.3) | copy-start | bytes 4718596
  0.6 3.0 %copy-start.1 = (f32[2,16,48,128]{3,2,1,0:T(8,128)S(1)}, f32[2,16,48,128]{3,2,1,0:T(8,128)}, u32[]{:S(2)}) copy-start(f32[2,16,48,128]{3,2,1,0:T(8,128)} %s_ref.3) | copy-start | bytes 2359300
  0.6 33.6 %collective-permute-start.1 = (f32[2,2,16,48,128]{4,3,2,1,0:T(8,128)}, f32[2,2,16,48,128]{4,3,2,1,0:T(8,128)S(1)}, u32[]{:S(2)}, u32[]{:S(2)}) collective-permute-start(f32[2,2,16,48,128]{4,3,2,1,0:T(8,128)} %k_ref.3), channel_id=1, source_target_pairs={{1,0},{0,1},{3,2},{2,3},{5,4},{4,5},{7,6},{6,7},{9,8},{8,9},{11,10... | collective-permute-start | bytes 4718600 | tf_op jit(solution)/shard_map/ppermute | solution.py:494
  1.2 1.1 %copy-start.2 = (f32[16,48,128]{2,1,0:T(8,128)S(1)}, f32[16,48,128]{2,1,0:T(8,128)}, u32[]{:S(2)}) copy-start(f32[16,48,128]{2,1,0:T(8,128)} %st_ref.3) | copy-start | bytes 1179652
  3.9 7.5 %collective-permute-start.8 = (f32[28,8,128]{2,1,0:T(8,128)S(1)}, f32[28,8,128]{2,1,0:T(8,128)S(1)}, u32[]{:S(2)}, u32[]{:S(2)}) collective-permute-start(f32[28,8,128]{2,1,0:T(8,128)S(1)} %get-tuple-element.31.mine), channel_id=1, source_target_pairs={{0,1},{1,0},{2,3},{3,2},{4,5},{5,4},{6,7},{7,6},{8,9},{9,8},{10,11... | collective-permute-start | bytes 344072 | tf_op jit(solution)/shard_map/ppermute | solution.py:489
  4.0 15.8 %collective-permute-start.4 = (f32[40,8,128]{2,1,0:T(8,128)S(1)}, f32[40,8,128]{2,1,0:T(8,128)S(1)}, u32[]{:S(2)}, u32[]{:S(2)}) collective-permute-start(f32[40,8,128]{2,1,0:T(8,128)S(1)} %get-tuple-element.26), channel_id=1, source_target_pairs={{0,6},{1,7},{2,0},{3,1},{4,2},{5,3},{6,4},{7,5},{8,14},{9,15},{10,... | collective-permute-start | bytes 491528 | tf_op jit(solution)/shard_map/ppermute | solution.py:486
  8.9 18.0 %collective-permute-start.7 = (f32[17,48,128]{2,1,0:T(8,128)S(1)}, f32[17,48,128]{2,1,0:T(8,128)S(1)}, u32[]{:S(2)}, u32[]{:S(2)}) collective-permute-start(f32[17,48,128]{2,1,0:T(8,128)S(1)} %get-tuple-element.24.zdn), channel_id=1, source_target_pairs={{0,24},{1,25},{2,26},{3,27},{4,28},{5,29},{6,30},{7,31},{8,0},{9,1... | collective-permute-start | bytes 1253384 | tf_op jit(solution)/shard_map/ppermute | solution.py:486
  11.4 6.2 %collective-permute-start.3 = (f32[20,8,128]{2,1,0:T(8,128)S(1)}, f32[20,8,128]{2,1,0:T(8,128)S(1)}, u32[]{:S(2)}, u32[]{:S(2)}) collective-permute-start(f32[20,8,128]{2,1,0:T(8,128)S(1)} %get-tuple-element.25), channel_id=1, source_target_pairs={{0,2},{1,3},{2,4},{3,5},{4,6},{5,7},{6,0},{7,1},{8,10},{9,11},{10,... | collective-permute-start | bytes 245768 | tf_op jit(solution)/shard_map/ppermute | solution.py:486
  11.4 22.9 %collective-permute-start = (f32[2,16,48,128]{3,2,1,0:T(8,128)S(1)}, f32[2,16,48,128]{3,2,1,0:T(8,128)S(1)}, u32[]{:S(2)}, u32[]{:S(2)}) collective-permute-start(f32[2,16,48,128]{3,2,1,0:T(8,128)S(1)} %copy-done.1), channel_id=1, source_target_pairs={{1,0},{0,1},{3,2},{2,3},{5,4},{4,5},{7,6},{6,7},{9,8},{8,9},{11,10... | collective-permute-start | bytes 2359304 | tf_op jit(solution)/shard_map/ppermute | solution.py:494
  17.6 6.1 %collective-permute-start.9 = (f32[18,8,128]{2,1,0:T(8,128)S(1)}, f32[18,8,128]{2,1,0:T(8,128)S(1)}, u32[]{:S(2)}, u32[]{:S(2)}) collective-permute-start(f32[18,8,128]{2,1,0:T(8,128)S(1)} %get-tuple-element.32), channel_id=1, source_target_pairs={{0,30},{1,11},{2,24},{3,13},{4,26},{5,15},{6,28},{7,9},{8,6},{9,19... | collective-permute-start | bytes 221192 | tf_op jit(solution)/shard_map/ppermute | solution.py:486
  19.7 7.2 %collective-permute-start.10 = (f32[18,8,128]{2,1,0:T(8,128)S(1)}, f32[18,8,128]{2,1,0:T(8,128)S(1)}, u32[]{:S(2)}, u32[]{:S(2)}) collective-permute-start(f32[18,8,128]{2,1,0:T(8,128)S(1)} %get-tuple-element.33), channel_id=1, source_target_pairs={{0,26},{1,15},{2,28},{3,9},{4,30},{5,11},{6,24},{7,13},{8,2},{9,23... | collective-permute-start | bytes 221192 | tf_op jit(solution)/shard_map/ppermute | solution.py:486
  23.7 8.6 %collective-permute-start.6 = (f32[10,48,128]{2,1,0:T(8,128)S(1)}, f32[10,48,128]{2,1,0:T(8,128)S(1)}, u32[]{:S(2)}, u32[]{:S(2)}) collective-permute-start(f32[10,48,128]{2,1,0:T(8,128)S(1)} %get-tuple-element.23.zup), channel_id=1, source_target_pairs={{0,8},{1,9},{2,10},{3,11},{4,12},{5,13},{6,14},{7,15},{8,16},{9,17... | collective-permute-start | bytes 737288 | tf_op jit(solution)/shard_map/ppermute | solution.py:486
  26.9 7.0 %collective-permute-start.2 = (f32[16,48,128]{2,1,0:T(8,128)S(1)}, f32[16,48,128]{2,1,0:T(8,128)S(1)}, u32[]{:S(2)}, u32[]{:S(2)}) collective-permute-start(f32[16,48,128]{2,1,0:T(8,128)S(1)} %copy-done.2), channel_id=1, source_target_pairs={{1,0},{0,1},{3,2},{2,3},{5,4},{4,5},{7,6},{6,7},{9,8},{8,9},{11,10... | collective-permute-start | bytes 1179656 | tf_op jit(solution)/shard_map/ppermute | solution.py:494
  26.9 11.4 %collective-permute-start.13 = (f32[17,48,128]{2,1,0:T(8,128)S(1)}, f32[17,48,128]{2,1,0:T(8,128)S(1)}, u32[]{:S(2)}, u32[]{:S(2)}) collective-permute-start(f32[17,48,128]{2,1,0:T(8,128)S(1)} %collective-permute-done.7.refs_5_), channel_id=1, source_target_pairs={{1,0},{0,1},{3,2},{2,3},{5,4},{4,5},{7,6},{6,7},{9,8},{8,9},{11,10... | collective-permute-start | bytes 1253384 | tf_op jit(solution)/shard_map/ppermute | solution.py:494
  32.4 1.4 %collective-permute-start.11 = (f32[36,8,128]{2,1,0:T(8,128)S(1)}, f32[36,8,128]{2,1,0:T(8,128)S(1)}, u32[]{:S(2)}, u32[]{:S(2)}) collective-permute-start(f32[36,8,128]{2,1,0:T(8,128)S(1)} %shard_map.52.got), channel_id=1, source_target_pairs={{0,1},{1,0},{2,3},{3,2},{4,5},{5,4},{6,7},{7,6},{8,9},{9,8},{10,11... | collective-permute-start | bytes 442376 | tf_op jit(solution)/shard_map/ppermute | solution.py:489
  33.7 1.8 %collective-permute-start.5 = (f32[60,8,128]{2,1,0:T(8,128)S(1)}, f32[60,8,128]{2,1,0:T(8,128)S(1)}, u32[]{:S(2)}, u32[]{:S(2)}) collective-permute-start(f32[60,8,128]{2,1,0:T(8,128)S(1)} %shard_map.50.refs_3_), channel_id=1, source_target_pairs={{1,0},{0,1},{3,2},{2,3},{5,4},{4,5},{7,6},{6,7},{9,8},{8,9},{11,10... | collective-permute-start | bytes 737288 | tf_op jit(solution)/shard_map/ppermute | solution.py:494
  33.9 4.4 %collective-permute-start.12 = (f32[10,48,128]{2,1,0:T(8,128)S(1)}, f32[10,48,128]{2,1,0:T(8,128)S(1)}, u32[]{:S(2)}, u32[]{:S(2)}) collective-permute-start(f32[10,48,128]{2,1,0:T(8,128)S(1)} %collective-permute-done.6.refs_4_), channel_id=1, source_target_pairs={{1,0},{0,1},{3,2},{2,3},{5,4},{4,5},{7,6},{6,7},{9,8},{8,9},{11,10... | collective-permute-start | bytes 737288 | tf_op jit(solution)/shard_map/ppermute | solution.py:494
